TPU v7x, 32 devices: a whole 2x2x4 slice. The times are simulated.
32 devices in a mesh: job: 2 (over y), ta: 4 (over z), xyz: 2 (over x), src: 2 (over core).
Axes of the slice: x: 2, y: 2, z: 4, core: 2. Of those that a mesh axis runs over, the one named last changes fastest.
Arguments:
- spinors: float32 [64, 8, 2, 8, 3, 512], P('src', 'ta', None, 'job', None, 'xyz'), parts along dimension 3, may hold values from -6 to 6
- eigvecs: float32 [8, 256, 2, 3, 512], P('ta', 'job', None, None, 'xyz'), parts along dimension 1, may hold values from -0.109375 to 0.109375
- group_of: int32 [8], replicated, may hold values from 0 to 3, as said below
- source_ids: int32 [64], P('src'), may hold values from 0 to 63, as said below
Outputs:
- perambulator: float32 [8, 2, 8, 64, 128], P('ta', None, 'job', 'src', 'xyz'), parts along dimension 2
There are 2 independent parts, one for each index of `job`. A program takes and returns all parts, laid end to end along the dimension named above; an argument that names none is the same for every part. Nothing has to cross between parts.
Inputs may be any that keep to these rules, and one draw needn't show every extreme that they name: `group_of`: every group number appears exactly 2 times. `source_ids`: the 32 entries held by index i of src are a permutation of i * 32 to (i + 1) * 32 - 1.
All inputs are finite; a program needn't handle non-finite values.
Results may differ from a plain program's by a relative error of at most 0.00007.
Values sent between devices are 32-bit elements; how exact they have to be, the bound alone decides.
A program may use at most 64 MiB of HBM per device.

v0:
```python
import jax
import jax.numpy as jnp
from jax import lax
from jax.sharding import PartitionSpec as P


def contract_pair(vectors, spinor):
    vector_real = vectors[:, :, 0]
    vector_imag = vectors[:, :, 1]
    spinor_real = spinor[:, :, 0]
    spinor_imag = spinor[:, :, 1]

    def contract(left_side, right_side):
        return jnp.einsum(
            "tkcx,ntscx->tsnk", left_side, right_side, precision=lax.Precision.HIGHEST
        )

    real_part = contract(vector_real, spinor_real) + contract(vector_imag, spinor_imag)
    imag_part = contract(vector_real, spinor_imag) - contract(vector_imag, spinor_real)
    return jnp.stack([real_part, imag_part], axis=1)


def local(spinors, eigvecs, group_of, source_ids):
    extent = group_of.shape[0]
    sort_keys = group_of * extent + jnp.arange(extent, dtype=jnp.int32)
    ordering = jnp.argsort(sort_keys)
    spread = lax.all_to_all(spinors, "ta", split_axis=0, concat_axis=1, tiled=True)
    grouped = jnp.take(spread, ordering, axis=1)
    regrouped = lax.all_to_all(grouped, "ta", split_axis=1, concat_axis=0, tiled=True)
    partial_sums = contract_pair(eigvecs, regrouped)
    summed = lax.psum_scatter(partial_sums, "xyz", scatter_dimension=4, tiled=True)
    inverse = jnp.argsort(source_ids)
    return jnp.take(summed, inverse, axis=3)


def solution(mesh):
    in_specs = (
        P("src", "ta", None, "job", None, "xyz"),
        P("ta", "job", None, None, "xyz"),
        P(),
        P("src"),
    )
    out_specs = P("ta", None, "job", "src", "xyz")
    return jax.shard_map(local, mesh=mesh, in_specs=in_specs, out_specs=out_specs, check_vma=False)
```

profile of v0, /device:TPU:0, one launch (start us, length us, event | category | flops | bytes accessed | tf_op | source)
XLA Modules:
  0.0 120.4 jit_solution(10331369571114613765)
XLA Ops:
  6.5 6.5 %all-to-all-start = ((f32[32,2,2,4,3,256]{5,3,4,2,1,0:T(4,128)}), f32[32,2,2,4,3,256]{5,3,4,2,1,0:T(4,128)S(1)}, u32[]{:S(2)}, u32[]{:S(2)}) async-start(f32[32,2,2,4,3,256]{5,3,4,2,1,0:T(4,128)} %param.4), calls=%async_computation | async-start | bytes 3145728 | tf_op jit(solution)/shard_map/all_to_all | solution.py:27
  13.0 1.0 sort.35
  14.0 36.0 %all-to-all-done = f32[32,2,2,4,3,256]{5,3,4,2,1,0:T(4,128)S(1)} async-done(((f32[32,2,2,4,3,256]{5,3,4,2,1,0:T(4,128)}), f32[32,2,2,4,3,256]{5,3,4,2,1,0:T(4,128)S(1)}, u32[]{:S(2)}, u32[]{:S(2)}) %all-to-all-start) | async-done | bytes 1572896 | tf_op jit(solution)/shard_map/all_to_all | solution.py:27
  50.0 0.9 copy.55
  50.9 0.2 copy.29
  51.1 0.7 gather_fusion
  51.7 1.4 %select_bitcast_fusion = f32[8,8,2,4,3,256]{5,0,4,3,2,1:T(8,128)} fusion(f32[8,8,2,4,3,256]{5,1,4,3,2,0:T(8,128)S(1)} %gather_fusion, pred[8]{0:T(512)(128)(4,1)S(1)} %compare_and_fusion), kind=kLoop, calls=%fused_computation.4 | loop fusion | flops 393216 | bytes 3145736 | tf_op jit(solution)/shard_map/jit(_take)/select_n | solution.py:28
  53.2 3.7 %all-to-all-start.1 = ((f32[8,8,2,4,3,256]{5,0,4,3,2,1:T(8,128)}), f32[8,8,2,4,3,256]{5,0,4,3,2,1:T(8,128)S(1)}, u32[]{:S(2)}, u32[]{:S(2)}) async-start(f32[8,8,2,4,3,256]{5,0,4,3,2,1:T(8,128)} %select_bitcast_fusion), calls=%async_computation.1 | async-start | bytes 3145728 | tf_op jit(solution)/shard_map/all_to_all | solution.py:29
  56.9 1.6 %sort.34 = (s32[32]{0:T(128)}, s32[32]{0:T(128)S(1)}) sort(s32[32]{0:T(128)S(1)} %copy-done.1, s32[32]{0:T(128)S(1)} %iota.11), dimensions={0}, to_apply=%region_0.0 | sort | flops 160 | bytes 512 | tf_op jit(solution)/shard_map/jit(argsort)/sort | solution.py:32
  58.5 3.4 %fusion.4 = (f32[2,128,1,3,256]{4,2,3,1,0:T(1,128)S(1)}, f32[2,128,1,3,256]{4,2,3,1,0:T(1,128)S(1)}) fusion(f32[2,128,2,3,256]{4,2,3,1,0:T(2,128)} %param.5), kind=kLoop, calls=%fused_computation.26 | loop fusion | bytes 3145728 | tf_op jit(solution)/shard_map/slice | solution.py:8
  61.9 31.4 %all-to-all-done.1 = f32[8,8,2,4,3,256]{5,0,4,3,2,1:T(8,128)S(1)} async-done(((f32[8,8,2,4,3,256]{5,0,4,3,2,1:T(8,128)}), f32[8,8,2,4,3,256]{5,0,4,3,2,1:T(8,128)S(1)}, u32[]{:S(2)}, u32[]{:S(2)}) %all-to-all-start.1) | async-done | bytes 1572896 | tf_op jit(solution)/shard_map/all_to_all | solution.py:29
  93.3 0.2 copy.54
  93.6 0.9 convolution_bitcast_fusion.2
  94.5 0.9 convolution_bitcast_fusion
  95.3 0.9 fusion.1
  96.2 0.9 fusion.3
  97.1 0.6 copy.41
  97.7 1.7 %reshape.34 = f32[128,512]{1,0:T(8,128)} reshape(f32[128,2,2,4,32]{4,3,2,1,0:T(4,128)S(1)} %bitcast.76) | data formatting | bytes 524288
  99.5 11.0 %reduce-scatter.4.cloned.1.call-done = f32[64,512]{1,0:T(8,128)} async-done(((f32[128,512]{1,0:T(8,128)}), f32[64,512]{1,0:T(8,128)}) %reduce-scatter.4.cloned.1.call-update) | async-done | bytes 131088
  110.4 1.2 reshape.35
  111.6 0.3 copy.33
  111.9 0.7 gather_fusion.1
  112.7 0.1 select_bitcast_fusion.1
  112.8 0.8 copy.34
  (16 shorter events, 0.1 us)
Async XLA Ops:
  6.5 6.5 %copy-start = (s32[8]{0:T(128)S(1)}, s32[8]{0:T(128)}, u32[]{:S(2)}) copy-start(s32[8]{0:T(128)} %param.6) | copy-start | bytes 100
  6.5 43.4 %all-to-all-start = ((f32[32,2,2,4,3,256]{5,3,4,2,1,0:T(4,128)}), f32[32,2,2,4,3,256]{5,3,4,2,1,0:T(4,128)S(1)}, u32[]{:S(2)}, u32[]{:S(2)}) async-start(f32[32,2,2,4,3,256]{5,3,4,2,1,0:T(4,128)} %param.4), calls=%async_computation | async-start | bytes 3145728 | tf_op jit(solution)/shard_map/all_to_all | solution.py:27
  53.1 3.8 %copy-start.1 = (s32[32]{0:T(128)S(1)}, s32[32]{0:T(128)}, u32[]{:S(2)}) copy-start(s32[32]{0:T(128)} %param.7) | copy-start | bytes 388
  53.2 40.2 %all-to-all-start.1 = ((f32[8,8,2,4,3,256]{5,0,4,3,2,1:T(8,128)}), f32[8,8,2,4,3,256]{5,0,4,3,2,1:T(8,128)S(1)}, u32[]{:S(2)}, u32[]{:S(2)}) async-start(f32[8,8,2,4,3,256]{5,0,4,3,2,1:T(8,128)} %select_bitcast_fusion), calls=%async_computation.1 | async-start | bytes 3145728 | tf_op jit(solution)/shard_map/all_to_all | solution.py:29
  56.9 53.6 %reduce-scatter.4.cloned.1.call-start = ((), (), s32[]{:S(2)}) async-start(), calls=%async_computation.3 | async-start | bytes 393216
Sparse Core Ops, SparseCore 0:
  99.5 10.8 reduce-scatter.3
where the time goes:
time: 121 us; the launch traced here: 120 us
  waiting for transfers between devices  78.4 us (65%)
  between operations  13.6 us (11%)
  local copies, waits for them, and re-layouts  10.6 us (9%)
  starting transfers between devices  10.2 us (8%)
  other arithmetic  4.16 us (3%)
  matrix products  3.51 us (3%)
    all_to_all x1, waiting for transfers between devices, local(): lax.all_to_all(spinors, 'ta', split_axis=0, concat_axis=1, tiled=True)  36 us
    all_to_all x1, waiting for transfers between devices, local(): lax.all_to_all(grouped, 'ta', split_axis=1, concat_axis=0, tiled=True)  31.4 us
    unnamed x2, waiting for transfers between devices  11 us
    all_to_all x1, starting transfers between devices, local(): lax.all_to_all(spinors, 'ta', split_axis=0, concat_axis=1, tiled=True)  6.48 us
    all_to_all x1, starting transfers between devices, local(): lax.all_to_all(grouped, 'ta', split_axis=1, concat_axis=0, tiled=True)  3.69 us
    dot_general x4, matrix products, contract(): jnp.einsum('tkcx,ntscx->tsnk', left_side, right_side, precision=lax.Preci...  3.51 us
    unnamed x7, local copies, waits for them, and re-layouts  3.43 us
    slice x1, local copies, waits for them, and re-layouts, contract_pair(): vector_real = vectors[:, :, 0]  3.37 us
  transfers between devices with their start and end apart: 3, of which 3 were waited for; matrix products, arithmetic and copies ran while one was open for 5% of the time, Pallas kernels for 0%

commit v1 on v0

--- a/solution.py
+++ b/solution.py
@@ -1,7 +1,14 @@
+import functools
+
 import jax
 import jax.numpy as jnp
 from jax import lax
+from jax.experimental import pallas as pl
+from jax.experimental.pallas import tpu as pltpu
 from jax.sharding import PartitionSpec as P
+
+MESH = pl.DeviceIdType.MESH
+OUT_PIECES = 2
 
 
 def contract_pair(vectors, spinor):
@@ -20,7 +27,7 @@
     return jnp.stack([real_part, imag_part], axis=1)
 
 
-def local(spinors, eigvecs, group_of, source_ids):
+def local_general(spinors, eigvecs, group_of, source_ids):
     extent = group_of.shape[0]
     sort_keys = group_of * extent + jnp.arange(extent, dtype=jnp.int32)
     ordering = jnp.argsort(sort_keys)
@@ -33,6 +40,319 @@
     return jnp.take(summed, inverse, axis=3)
 
 
+def copy_to(src, dst, sems, index, where):
+    return pltpu.make_async_remote_copy(
+        src_ref=src,
+        dst_ref=dst,
+        send_sem=sems.at[0, index],
+        recv_sem=sems.at[1, index],
+        device_id=where,
+        device_id_type=MESH,
+    )
+
+
+def kernel(n, m, pieces, tab, e_ref, s_ref, out_ref, *scratch):
+    held = e_ref.shape[0]
+    scratch = list(scratch)
+
+    def take(count):
+        got = scratch[:count]
+        del scratch[:count]
+        return got
+
+    side_e, mid_e, recv_e, give_e = take(pieces), take(pieces), take(pieces), take(pieces)
+    side_o, mid_o, recv_o, give_o = (
+        take(OUT_PIECES), take(OUT_PIECES), take(OUT_PIECES), take(OUT_PIECES)
+    )
+    full, high, low, acc, x_recv, o_recv, o_send = take(7)
+    in_e, cross_e, back_e, core_e, x_sem, in_o, cross_o, back_o = take(8)
+
+    z = lax.axis_index("ta")
+    core = lax.axis_index("src")
+    xi = lax.axis_index("xyz")
+    right = z // (n // 2)
+    inner = jnp.logical_and(z > 0, z < n - 1)
+    outer = jnp.logical_not(inner)
+    to_inner = {"ta": 1 + right}
+    to_outer = {"ta": right * (n - 1)}
+    to_other = {"ta": n - 1 - z}
+    to_core = {"src": 1 - core}
+    to_x = {"xyz": 1 - xi}
+    outer_at = right * held
+    own_at = (1 - right) * held
+    depth = e_ref.shape[2] // 2
+    half_rows = pl.ds(pl.multiple_of(core * depth, depth), depth)
+    other_rows = pl.ds(pl.multiple_of((1 - core) * depth, depth), depth)
+
+    barrier = pltpu.get_barrier_semaphore()
+    for where in (to_core, to_x):
+        pl.semaphore_signal(barrier, inc=1, device_id=where, device_id_type=MESH)
+
+    @pl.when(inner)
+    def _():
+        for where in (to_outer, to_other):
+            pl.semaphore_signal(barrier, inc=1, device_id=where, device_id_type=MESH)
+        pl.semaphore_wait(barrier, 4)
+
+    @pl.when(outer)
+    def _():
+        pl.semaphore_signal(barrier, inc=1, device_id=to_inner, device_id_type=MESH)
+        pl.semaphore_wait(barrier, 3)
+
+    def mine(j):
+        return e_ref.at[:, j, half_rows, :]
+
+    def inward_e(j):
+        return copy_to(mine(j), side_e[j].at[pl.ds(outer_at, held)], in_e, j, to_inner)
+
+    def across_e(j):
+        return copy_to(mid_e[j], recv_e[j], cross_e, j, to_other)
+
+    def back_out_e(j):
+        return copy_to(give_e[j], full.at[j, :, half_rows, :], back_e, j, to_outer)
+
+    def swap_e(j):
+        view = full.at[j, :, half_rows, :]
+        return copy_to(view, view, core_e, j, to_core)
+
+    def swapped_e(j):
+        view = full.at[j, :, other_rows, :]
+        return copy_to(view, view, core_e, j, to_core)
+
+    def chosen(which, q, side, recv):
+        own = side[tab[which, 1, q]]
+        far = recv[tab[which, 2, q]]
+        return jnp.where(tab[which, 3, q] == 1, own, far)
+
+    @pl.when(outer)
+    def _():
+        for j in range(pieces):
+            inward_e(j).start()
+
+    @pl.when(inner)
+    def _():
+        for j in range(pieces):
+            side_e[j][pl.ds(own_at, held)] = e_ref[:, j, half_rows, :]
+
+    def split(value):
+        top = value.astype(jnp.bfloat16)
+        return top, (value - top.astype(jnp.float32)).astype(jnp.bfloat16)
+
+    colours = s_ref.shape[2]
+    width = s_ref.shape[3]
+
+    for t in range(held):
+        acc[t] = jnp.zeros(acc.shape[1:], jnp.float32)
+        for c in range(colours):
+            real_top, real_low = split(s_ref[t, 0, c])
+            imag_top, imag_low = split(s_ref[t, 1, c])
+            for keep, real, imag in ((high, real_top, imag_top), (low, real_low, imag_low)):
+                keep[t, 2 * c, :width] = real
+                keep[t, 2 * c, width:] = imag
+                keep[t, 2 * c + 1, :width] = imag
+                keep[t, 2 * c + 1, width:] = -real
+
+    @pl.when(inner)
+    def _():
+        def finish(j):
+            across_e(j).wait_recv()
+            for i in range(held):
+                give_e[j][i] = chosen(0, outer_at + i, side_e[j], recv_e[j])
+            back_out_e(j).start()
+            for i in range(held):
+                full[j, i, half_rows, :] = chosen(0, own_at + i, side_e[j], recv_e[j])
+            swap_e(j).start()
+
+        for j in range(pieces):
+            inward_e(j).wait_recv()
+            for slot in range(m):
+                mid_e[j][slot] = side_e[j][tab[0, 0, slot]]
+            across_e(j).start()
+            if j > 0:
+                finish(j - 1)
+        finish(pieces - 1)
+        for j in range(pieces):
+            across_e(j).wait_send()
+            back_out_e(j).wait_send()
+
+    @pl.when(outer)
+    def _():
+        for j in range(pieces):
+            back_out_e(j).wait_recv()
+            swap_e(j).start()
+        for j in range(pieces):
+            inward_e(j).wait_send()
+
+    for j in range(pieces):
+        swapped_e(j).wait_recv()
+
+    def step(j, carry):
+        for t in range(held):
+            top, rest = split(full[j, t])
+
+            def dot(a, b):
+                return lax.dot_general(
+                    a, b, (((1,), (1,)), ((), ())), preferred_element_type=jnp.float32
+                )
+
+            acc[t] += dot(top, high[t, j]) + (dot(top, low[t, j]) + dot(rest, high[t, j]))
+        return carry
+
+    lax.fori_loop(0, pieces, step, 0)
+    for j in range(pieces):
+        swap_e(j).wait_send()
+
+    rows = acc.shape[1] // 2
+    part = rows // OUT_PIECES
+
+    def x_swap(q):
+        there = pl.ds(pl.multiple_of((1 - xi) * rows + q * part, part), part)
+        return copy_to(acc.at[:, there, :], x_recv.at[q], x_sem, q, to_x)
+
+    def summed(q):
+        here = pl.ds(pl.multiple_of(xi * rows + q * part, part), part)
+        return acc[:, here, :] + x_recv[q]
+
+    def inward_o(q):
+        return copy_to(o_send.at[q], side_o[q].at[pl.ds(outer_at, held)], in_o, q, to_inner)
+
+    def across_o(q):
+        return copy_to(mid_o[q], recv_o[q], cross_o, q, to_other)
+
+    def back_out_o(q):
+        return copy_to(give_o[q], o_recv.at[q], back_o, q, to_outer)
+
+    for q in range(OUT_PIECES):
+        x_swap(q).start()
+
+    @pl.when(outer)
+    def _():
+        for q in range(OUT_PIECES):
+            x_swap(q).wait_recv()
+            o_send[q] = summed(q)
+            inward_o(q).start()
+        for q in range(OUT_PIECES):
+            back_out_o(q).wait_recv()
+            out_ref[:, q * part:(q + 1) * part, :] = o_recv[q]
+        for q in range(OUT_PIECES):
+            inward_o(q).wait_send()
+
+    @pl.when(inner)
+    def _():
+        for q in range(OUT_PIECES):
+            x_swap(q).wait_recv()
+            side_o[q][pl.ds(own_at, held)] = summed(q)
+        for q in range(OUT_PIECES):
+            inward_o(q).wait_recv()
+            for slot in range(m):
+                mid_o[q][slot] = side_o[q][tab[1, 0, slot]]
+            across_o(q).start()
+        for q in range(OUT_PIECES):
+            across_o(q).wait_recv()
+            for i in range(held):
+                give_o[q][i] = chosen(1, outer_at + i, side_o[q], recv_o[q])
+            back_out_o(q).start()
+            for i in range(held):
+                out_ref[i, q * part:(q + 1) * part, :] = chosen(
+                    1, own_at + i, side_o[q], recv_o[q]
+                )
+        for q in range(OUT_PIECES):
+            across_o(q).wait_send()
+            back_out_o(q).wait_send()
+
+    for q in range(OUT_PIECES):
+        x_swap(q).wait_send()
+
+
+def local_line(n, spinors, eigvecs, group_of, source_ids):
+    extent = group_of.shape[0]
+    half = extent // 2
+    sources, held, _, spins, colours, sites = spinors.shape
+    vectors = eigvecs.shape[1]
+    pieces = 2 * colours
+    depth = vectors // 2
+    width = spins * sources
+
+    items = jnp.arange(extent, dtype=jnp.int32)
+    keys = group_of * extent + items
+    rank = jnp.sum((keys[None, :] < keys[:, None]).astype(jnp.int32), axis=1)
+    match = rank[None, :] == items[:, None]
+    ordering = jnp.sum(jnp.where(match, items[None, :], 0), axis=1)
+    right = lax.axis_index("ta") // (n // 2)
+    spot = jnp.arange(half, dtype=jnp.int32)
+
+    def tables(wanted, goes_to):
+        crosses = (goes_to // half) != (items // half)
+        same = (items // half)[:, None] == (items // half)[None, :]
+        before = crosses[None, :] & same & (items[None, :] < items[:, None])
+        slot = jnp.sum(before.astype(jnp.int32), axis=1)
+        leaving = crosses & ((items // half) == right)
+        send = jnp.sum(
+            jnp.where(leaving[None, :] & (slot[None, :] == spot[:, None]), items[None, :] % half, 0),
+            axis=1,
+        )
+        here = items[None, :] == (spot + right * half)[:, None]
+        want = jnp.sum(jnp.where(here, wanted[None, :], 0), axis=1)
+        own = (want // half) == right
+        far = jnp.sum(jnp.where(items[None, :] == want[:, None], slot[None, :], 0), axis=1)
+        table = jnp.stack([
+            send,
+            jnp.where(own, want % half, 0),
+            jnp.where(own, 0, far),
+            own.astype(jnp.int32),
+        ])
+        return table, jnp.sum(jnp.where(items < half, crosses.astype(jnp.int32), 0))
+
+    table_e, count = tables(rank, ordering)
+    table_o, _ = tables(ordering, rank)
+    table = jnp.stack([table_e, table_o])
+
+    e_view = eigvecs.transpose(0, 3, 2, 1, 4).reshape(held, pieces, vectors, sites)
+    s_view = spinors.transpose(1, 2, 4, 3, 0, 5).reshape(held, 2, colours, width, sites)
+
+    rows = vectors // 2
+    part = rows // OUT_PIECES
+    f32 = jnp.float32
+
+    def run(m):
+        vmem = pl.BlockSpec(memory_space=pltpu.VMEM)
+        e_item = (depth, sites)
+        o_item = (part, 2 * width)
+        buffers = []
+        for count_, item in ((pieces, e_item), (OUT_PIECES, o_item)):
+            for slots in (half, m, m, held):
+                buffers += [pltpu.VMEM((slots,) + item, f32)] * count_
+        return pl.pallas_call(
+            functools.partial(kernel, n, m, pieces),
+            name=f"project_{m}",
+            out_shape=jax.ShapeDtypeStruct((held, rows, 2 * width), f32),
+            in_specs=[pl.BlockSpec(memory_space=pltpu.SMEM), vmem, vmem],
+            out_specs=vmem,
+            scratch_shapes=buffers + [
+                pltpu.VMEM((pieces, held, vectors, sites), f32),
+                pltpu.VMEM((held, pieces, 2 * width, sites), jnp.bfloat16),
+                pltpu.VMEM((held, pieces, 2 * width, sites), jnp.bfloat16),
+                pltpu.VMEM((held, vectors, 2 * width), f32),
+                pltpu.VMEM((OUT_PIECES, held) + o_item, f32),
+                pltpu.VMEM((OUT_PIECES, held) + o_item, f32),
+                pltpu.VMEM((OUT_PIECES, held) + o_item, f32),
+            ] + [pltpu.SemaphoreType.DMA((2, pieces))] * 4
+            + [pltpu.SemaphoreType.DMA((2, OUT_PIECES))] * 4,
+            compiler_params=pltpu.CompilerParams(
+                collective_id=m, has_side_effects=True, vmem_limit_bytes=48 * 1024 * 1024
+            ),
+        )
+
+    branches = [run(m) for m in range(1, half + 1)]
+    projected = lax.switch(jnp.maximum(count, 1) - 1, branches, table, e_view, s_view)
+    projected = projected.reshape(held, rows, 2, spins, sources)
+    first = lax.axis_index("src") * sources
+    place = (source_ids[None, :] - first) == jnp.arange(sources, dtype=jnp.int32)[:, None]
+    return jnp.einsum(
+        "jn,rkpsn->rpsjk", place.astype(f32), projected, precision=lax.Precision.HIGHEST
+    )
+
+
 def solution(mesh):
     in_specs = (
         P("src", "ta", None, "job", None, "xyz"),
@@ -41,4 +361,7 @@
         P("src"),
     )
     out_specs = P("ta", None, "job", "src", "xyz")
+    n = mesh.shape["ta"]
+    line = n == 4 and mesh.shape["src"] == 2 and mesh.shape["xyz"] == 2
+    local = functools.partial(local_line, n) if line else local_general
     return jax.shard_map(local, mesh=mesh, in_specs=in_specs, out_specs=out_specs, check_vma=False)

time: 121 us -> 56.8 us (0.47)
  waiting for transfers between devices: 78.4 us -> 0 us
  Pallas kernels: 0 us -> 49.3 us
  between operations: 13.6 us -> 0.75 us
  starting transfers between devices: 10.2 us -> 0 us
  local copies, waits for them, and re-layouts: 10.6 us -> 2.73 us
  matrix products: 3.51 us -> 0.96 us
  other arithmetic: 4.16 us -> 2.89 us
    all_to_all x2 -> x0, waiting for transfers between devices: 67.4 us -> none  [the longest x1 36 us: local(): lax.all_to_all(spinors, 'ta', split_axis=0, concat_axis=1, tiled=True)]
    pallas_call x0 -> x1, Pallas kernels: none -> 49.3 us  [local_line(): lax.switch(jnp.maximum(count, 1) - 1, branches, table, e_view, s_view)]
    unnamed x2 -> x0, waiting for transfers between devices: 11 us -> none
    all_to_all x2 -> x0, starting transfers between devices: 10.2 us -> none  [the longest x1 6.48 us: local(): lax.all_to_all(spinors, 'ta', split_axis=0, concat_axis=1, tiled=True)]
    slice x1 -> x0, local copies, waits for them, and re-layouts: 3.37 us -> none  [contract_pair(): vector_real = vectors[:, :, 0]]
    sort x2 -> x0, other arithmetic: 2.57 us -> none  [the longest x1 1.61 us: local(): inverse = jnp.argsort(source_ids)]
    dot_general x4 -> x1, matrix products: 3.51 us -> 0.96 us  [local_line(): jnp.einsum('jn,rkpsn->rpsjk', place.astype(f32), projected, precision=lax...]
    select_n x4, other arithmetic: 1.54 us -> 0.03 us  [the longest x2 0.03 us: tables(): jnp.where(own, want % half, 0)]
  transfers between devices with their start and end apart: 3 -> 0, of which waited for: 3 -> 0; matrix products, arithmetic and copies ran while one was open for 5% -> 0% of each run, Pallas kernels for 0% -> 0%
where the time goes in v1:
time: 56.8 us; the launch traced here: 56.7 us
  Pallas kernels  49.3 us (87%)
  other arithmetic  2.89 us (5%)
  local copies, waits for them, and re-layouts  2.73 us (5%)
  matrix products  0.96 us (2%)
  between operations  0.75 us (1%)
    pallas_call x1, Pallas kernels, local_line(): lax.switch(jnp.maximum(count, 1) - 1, branches, table, e_view, s_view)  49.3 us
    unnamed x4, local copies, waits for them, and re-layouts  2.61 us

profile of v1, /device:TPU:0, one launch (start us, length us, event | category | flops | bytes accessed | tf_op | source)
XLA Modules:
  0.0 56.7 jit_solution(3934634717499827464)
XLA Ops:
  0.0 0.7 %broadcast_subtract_fusion = s32[32]{0:T(128)S(1)} fusion(s32[32]{0:T(128)} %param.11, s32[]{:T(128)S(6)} %mul.12), kind=kLoop, calls=%fused_computation.71 | loop fusion | flops 32 | bytes 260 | tf_op jit(solution)/shard_map/sub | solution.py:350
  0.7 0.7 %iota_add_fusion.1 = s32[8]{0:T(128)S(1)} fusion(s32[8]{0:T(128)} %param.10), kind=kLoop, calls=%fused_computation.68 | loop fusion | flops 16 | bytes 64 | tf_op jit(solution)/shard_map/add | solution.py:277
  1.3 0.2 convert_reduce_fusion.2
  1.5 0.1 select_reduce_fusion
  1.6 0.2 select_reduce_fusion.5
  1.8 0.6 %fusion.9 = s32[]{:T(128)} fusion(pred[8]{0:T(512)(128)(4,1)S(1)} %get-tuple-element.72), kind=kLoop, calls=%fused_computation.60 | loop fusion | flops 31 | bytes 12 | tf_op jit(solution)/shard_map/reduce_sum | solution.py:304
  3.1 0.2 convert_reduce_fusion.1
  3.3 0.2 select_reduce_fusion.6
  3.6 0.0 copy-start
  3.6 2.4 %copy.23 = f32[32,2,2,4,3,256]{5,0,3,4,2,1:T(8,128)S(1)} copy(f32[32,2,2,4,3,256]{5,3,4,2,1,0:T(4,128)} %param.8) | data formatting | bytes 3145728 | tf_op args[0]
  6.1 0.0 copy-done
  6.1 0.2 copy.24
  6.2 49.5 %conditional.1 = (f32[2,64,2,4,32]{1,4,3,2,0:T(8,128)S(1)}) conditional(s32[]{:T(128)} %clamp.3, (f32[2,3,2,128,256]{4,3,2,1,0:T(8,128)S(1)}, f32[2,2,3,4,32,256]{5,4,3,2,1,0:T(8,128)S(1)}, s32[2,4,4]{2,1,0:T(4,128)S(1)}) %tuple.42, (f32[2,3,2,128,256]{4,3,2,1,0:T(8,128)S(1)}, ...), branch_computations={%region_11.12_spmd, %region_12.13_spmd, %region_13.14_spmd, %regio... | conditional | bytes 262152 | solution.py:347
  6.3 49.3 %project_1.1 = f32[2,64,256]{2,1,0:T(8,128)S(1)} custom-call(s32[2,4,4]{2,1,0:T(4,128)S(1)} %get-tuple-element.43.tab, f32[2,6,128,256]{3,2,1,0:T(8,128)S(1)} %bitcast.94, f32[2,2,3,128,256]{4,3,2,1,0:T(8,128)S(1)} %bitcast.86), custom_call_target="tpu_custom_call" | custom-call | tf_op jit(solution)/shard_map/cond/branch_0_fun/project_1/pallas_call | solution.py:347
  55.6 0.1 copy.14
  55.7 1.0 %convolution_bitcast_fusion = f32[2,2,4,32,64]{4,3,2,1,0:T(8,128)} fusion(f32[2,64,2,4,32]{1,4,3,2,0:T(8,128)S(1)} %get-tuple-element.75, s32[32]{0:T(128)S(1)} %broadcast_subtract_fusion), kind=kOutput, calls=%fused_computation.2 | convolution fusion | flops 12583936 | bytes 262272 | tf_op jit(solution)/shard_map/jn,rkpsn->rpsjk/dot_general | solution.py:351
  (10 shorter events, 0.1 us)
Async XLA Ops:
  3.6 2.5 %copy-start = (f32[2,128,2,3,256]{4,2,3,1,0:T(2,128)S(1)}, f32[2,128,2,3,256]{4,2,3,1,0:T(2,128)}, u32[]{:S(2)}) copy-start(f32[2,128,2,3,256]{4,2,3,1,0:T(2,128)} %param.9) | copy-start | bytes 4718596
